TPU v7x, 1024 devices: a whole 4x8x16 slice. The times are simulated.
1024 devices in a mesh: dp: 128 (over z, x, core), slab: 8 (over y).
Axes of the slice: x: 4, y: 8, z: 16, core: 2. Of those that a mesh axis runs over, the one named last changes fastest.
Arguments:
- inputs: bfloat16 [128, 48, 34944], P('dp', 'slab'), may hold values from -40 to 40
- upstream: bfloat16 [128, 48, 34944], P('dp', 'slab'), may hold values from -96 to 96
- labels: int32 [128, 48, 48], P('dp', 'slab'), may hold values from 0 to 2
- class_weights: float32 [3], replicated, may hold values from 0.25 to 4
- depth_kernel: bfloat16 [9, 728], replicated, may hold values from -2 to 2
- point_weight: bfloat16 [728, 728], replicated, may hold values from -0.21875 to 0.21875
- gain: float32 [728], replicated, may hold values from 0.5 to 1.5
- shift: float32 [728], replicated, may hold values from -3 to 3
Outputs:
- block_out: bfloat16 [128, 48, 34944], P('dp', 'slab')
- grad_input: bfloat16 [128, 48, 34944], P('dp', 'slab')
- grad_pointwise: float32 [728, 728], P(None, 'slab')
- grad_depthwise: float32 [9, 728], P(None, 'slab')
- grad_gain: float32 [728], P('slab')
- grad_shift: float32 [728], P('slab')
All inputs are finite; a program needn't handle non-finite values.
Results may differ from a plain program's by a relative error of at most 0.0052.
The roundings to bfloat16 on the way count: a program that leaves them out, or rounds other values in their place, can miss the bound.
Values may be sent and summed in bfloat16 or wider, within the bound.
A program may use at most 32 MiB of HBM per device.

v0:
```python
import jax
import jax.numpy as jnp
from jax import lax
from jax.sharding import PartitionSpec as P


def padded_2(cells, sides, width):
    for axis, dim in sides:
        count = lax.axis_size(axis)
        ends = count - 1
        head = lax.slice_in_dim(cells, 0, width, axis=dim)
        tail = lax.slice_in_dim(cells, cells.shape[dim] - width, cells.shape[dim], axis=dim)
        cells = jnp.concatenate(
            [
                lax.ppermute(tail, axis, [(i, (i + 1) % count) for i in range(ends)]),
                cells,
                lax.ppermute(head, axis, [((i + 1) % count, i) for i in range(ends)]),
            ],
            axis=dim,
        )
    return cells


def widen_columns(values):
    return jnp.pad(values, ((0, 0), (0, 0), (1, 1), (0, 0)))


def depthwise(padded, kernel):
    row_count = padded.shape[1] - 2
    col_count = padded.shape[2]
    widened = widen_columns(padded)
    summed = jnp.zeros((padded.shape[0], row_count, col_count, padded.shape[3]), jnp.float32)
    for row_tap in range(3):
        for col_tap in range(3):
            window = widened[:, row_tap : row_tap + row_count, col_tap : col_tap + col_count, :]
            summed = summed + window.astype(jnp.float32) * kernel[3 * row_tap + col_tap].astype(
                jnp.float32
            )
    return summed


def transposed(padded_grad, kernel):
    row_count = padded_grad.shape[1] - 2
    col_count = padded_grad.shape[2]
    widened = widen_columns(padded_grad)
    summed = jnp.zeros(
        (padded_grad.shape[0], row_count, col_count, padded_grad.shape[3]), jnp.float32
    )
    for row_tap in range(3):
        for col_tap in range(3):
            window = widened[
                :, 2 - row_tap : 2 - row_tap + row_count, 2 - col_tap : 2 - col_tap + col_count, :
            ]
            summed = summed + window.astype(jnp.float32) * kernel[3 * row_tap + col_tap].astype(
                jnp.float32
            )
    return summed


def taps(padded, grad_image):
    row_count = grad_image.shape[1]
    col_count = grad_image.shape[2]
    widened = widen_columns(padded)
    results = []
    for row_tap in range(3):
        for col_tap in range(3):
            window = widened[:, row_tap : row_tap + row_count, col_tap : col_tap + col_count, :]
            results.append(
                jnp.einsum("srwc,srwc->c", window, grad_image, preferred_element_type=jnp.float32)
            )
    return jnp.stack(results)


def rows_around(values):
    return padded_2(values, (("slab", 1),), 1)


def slab_totals(first, second):
    return lax.psum((first, second), "slab")


def local(inputs, upstream, labels, class_weights, depth_kernel, point_weight, gain, shift):
    samples, row_count, flat_width = inputs.shape
    channels = point_weight.shape[0]
    col_count = flat_width // channels
    pieces = lax.axis_size("slab")
    share = channels // pieces
    sample = inputs.reshape(samples, row_count, col_count, channels)
    active = jnp.maximum(sample, 0)
    padded = rows_around(active)
    depth = depthwise(padded, depth_kernel).astype(jnp.bfloat16)
    flat_depth = depth.reshape(-1, channels)
    projected = jnp.dot(flat_depth, point_weight, preferred_element_type=jnp.float32)
    match = labels.reshape(-1)[:, None] == jnp.arange(3, dtype=jnp.int32)[None, :]
    weight = jnp.sum(jnp.where(match, class_weights[None, :], 0.0), axis=1)
    grad_out = upstream.reshape(-1, channels).astype(jnp.float32) * weight[:, None]
    count = projected.shape[0] * pieces
    proj_sum, shift_part = slab_totals(jnp.sum(projected, axis=0), jnp.sum(grad_out, axis=0))
    center = proj_sum / count
    deviation = projected - center
    square_sum, cross = slab_totals(
        jnp.sum(deviation * deviation, axis=0), jnp.sum(grad_out * deviation, axis=0)
    )
    spread = square_sum / count
    inverse = lax.rsqrt(spread + 1e-05)
    normed = (projected - center) * inverse
    gain_part = cross * inverse
    result = sample.reshape(-1, channels).astype(jnp.float32) + gain * normed + shift
    grad_proj = (
        gain * inverse * (grad_out - shift_part / count - normed * gain_part / count)
    ).astype(jnp.bfloat16)
    grad_depth = lax.dot_general(
        grad_proj, point_weight, (((1,), (1,)), ((), ())), preferred_element_type=jnp.float32
    ).astype(jnp.bfloat16)
    grad_image = grad_depth.reshape(depth.shape)
    padded_grad = rows_around(grad_image)
    grad_active = transposed(padded_grad, depth_kernel).reshape(-1, channels)
    grad_input = grad_out + jnp.where(sample.reshape(-1, channels) > 0, grad_active, 0.0)
    tap_local = taps(padded, grad_image)
    point_local = lax.dot_general(
        flat_depth, grad_proj, (((0,), (0,)), ((), ())), preferred_element_type=jnp.float32
    )
    point_share, tap_share = (
        lax.psum_scatter(point_local, "slab", scatter_dimension=1, tiled=True),
        lax.psum_scatter(tap_local, "slab", scatter_dimension=1, tiled=True),
    )
    offset = lax.axis_index("slab") * share
    gain_share = lax.dynamic_slice_in_dim(gain_part, offset, share, 0)
    shift_share = lax.dynamic_slice_in_dim(shift_part, offset, share, 0)
    point_sum, tap_sum, gain_sum, shift_sum = lax.psum(
        (point_share, tap_share, gain_share, shift_share), "dp"
    )
    batch = samples * lax.axis_size("dp")
    block_out = result.astype(jnp.bfloat16).reshape(samples, row_count, flat_width)
    grad_in = grad_input.astype(jnp.bfloat16).reshape(samples, row_count, flat_width)
    return (
        block_out,
        grad_in,
        point_sum / batch,
        tap_sum / batch,
        gain_sum / batch,
        shift_sum / batch,
    )


def solution(mesh):
    return jax.shard_map(
        local,
        mesh=mesh,
        in_specs=(
            P("dp", "slab", None),
            P("dp", "slab", None),
            P("dp", "slab", None),
            P(),
            P(),
            P(),
            P(),
            P(),
        ),
        out_specs=(
            P("dp", "slab", None),
            P("dp", "slab", None),
            P(None, "slab"),
            P(None, "slab"),
            P("slab"),
            P("slab"),
        ),
        check_vma=False,
    )
```

profile of v0, /device:TPU:1, one launch (start us, length us, event | category | flops | bytes accessed | tf_op | source)
XLA Modules:
  0.0 789.9 jit_solution(17338108056016282103)
XLA Ops:
  10.3 4.0 collective-permute-start
  15.6 2.0 reshape.238
  17.6 1.9 max.28
  22.4 1.7 mul.233
  24.1 1.3 fusion.18
  29.5 1.4 fusion.19
  30.9 14.8 %psum.56 = f32[728]{0:T(1024)S(1)} all-reduce(f32[728]{0:T(1024)S(1)} %get-tuple-element.46), channel_id=1, replica_groups=mesh['dp'=128,'slab'=8] {'slab'}, use_global_device_ids=true, to_apply=%region_1.2 | all-reduce | flops 728 | bytes 5824 | tf_op jit(solution)/shard_map/psum | solution.py:79
  45.7 1.4 multiply_reduce_fusion
  47.1 21.7 %all-reduce.6 = (f32[728]{0:T(1024)S(1)}, f32[728]{0:T(1024)S(1)}, f32[728]{0:T(1024)S(1)}) all-reduce(f32[728]{0:T(1024)S(1)} %get-tuple-element.13, f32[728]{0:T(1024)S(1)} %get-tuple-element.12, f32[728]{0:T(1024)S(1)} %get-tuple-element.14), channel_id=1, replica_groups=mesh['dp'=128,'slab'=8] {'slab'}, use_global_device_ids=true, to_apply=%region_3.4 | all-reduce | flops 2184 | bytes 17472 | tf_op jit(solution)/shard_map/psum | solution.py:79
  69.0 2.6 multiply_convert_fusion
  72.6 2.1 fusion.20
  75.7 20.5 %all-reduce.3 = f32[9,728]{1,0:T(8,128)S(1)} all-reduce(f32[9,728]{1,0:T(8,128)S(1)} %stack.39), channel_id=3, replica_groups=mesh['dp'=128,'slab'=8] {'slab'}, use_global_device_ids=true, to_apply=%region_11.12.clone | all-reduce | flops 6552 | bytes 52416
  96.3 286.7 %all-reduce.5 = (f32[9,91]{1,0:T(8,128)S(1)}, f32[91]{0:T(128)S(1)}, f32[91]{0:T(128)S(1)}) all-reduce(f32[9,91]{1,0:T(8,128)S(1)} %constant_dynamic-slice_fusion.1, f32[91]{0:T(128)S(1)} %dynamic_slice.6, f32[91]{0:T(128)S(1)} %dynamic_slice.7), channel_id=1, replica_groups=mesh['dp'=128,'slab'=8] {'dp'}, use_global_device_ids=true, to_apply=%region_12.13 | all-reduce | flops 1001 | bytes 8008 | tf_op jit(solution)/shard_map/psum | solution.py:130
  384.1 32.1 %fusion = f32[728,96]{0,1:T(8,128)S(1)} fusion(f32[728,728]{0,1:T(8,128)} %fusion.20), kind=kCustom, calls=%all-reduce-scatter | all-reduce-scatter fusion | flops 559105 | bytes 2403584
  416.3 2.1 collective-permute-start.2
  420.8 4.2 collective-permute-start.4
  425.0 1.7 reshape.226
  426.9 1.6 multiply_add_fusion
  428.5 3.1 reshape.228
  431.6 2.4 concatenate.24
  434.0 1.7 constant_dynamic-slice_fusion
  435.8 2.4 add_convert_fusion
  438.2 343.2 %all-reduce.9.cloned.1.call-done = f32[728,91]{0,1:T(8,128)} async-done(((f32[728,91]{0,1:T(8,128)}), f32[728,91]{0,1:T(8,128)}) %all-reduce.9.cloned.1.call-update) | async-done | bytes 265008 | tf_op jit(solution)/shard_map/psum | solution.py:130
  781.4 1.7 broadcast_multiply_fusion
  (74 shorter events, 15.9 us)
Async XLA Ops:
  7.2 22.3 %copy-start = (bf16[728,728]{1,0:T(8,128)(2,1)S(1)}, bf16[728,728]{1,0:T(8,128)(2,1)}, u32[]{:S(2)}) copy-start(bf16[728,728]{1,0:T(8,128)(2,1)} %param.13) | copy-start | bytes 3179908
  7.2 8.4 %copy-start.1 = (bf16[1,6,34944]{2,1,0:T(8,128)(2,1)S(1)}, bf16[1,6,34944]{2,1,0:T(8,128)(2,1)}, u32[]{:S(2)}) copy-start(bf16[1,6,34944]{2,1,0:T(8,128)(2,1)} %param.8) | copy-start | bytes 1257988
  7.2 774.2 %all-reduce.9.cloned.1.call-start = ((), (), s32[]{:S(2)}) async-start(), calls=%async_computation | async-start | bytes 589824 | tf_op jit(solution)/shard_map/psum | solution.py:130
  9.6 9.9 %copy-start.13 = (s32[1,6,48]{2,0,1:T(1,128)S(1)}, s32[1,6,48]{2,0,1:T(1,128)}, u32[]{:S(2)}) copy-start(s32[1,6,48]{2,0,1:T(1,128)} %param.10) | copy-start | bytes 3460
  9.6 10.0 %copy-start.6 = (bf16[1,6,34944]{2,1,0:T(8,128)(2,1)S(1)}, bf16[1,6,34944]{2,1,0:T(8,128)(2,1)}, u32[]{:S(2)}) copy-start(bf16[1,6,34944]{2,1,0:T(8,128)(2,1)} %param.9) | copy-start | bytes 1257988
  10.3 17.5 %collective-permute-start = (bf16[1,1,48,728]{3,2,1,0:T(8,128)(2,1)}, bf16[1,1,48,728]{3,2,1,0:T(8,128)(2,1)S(1)}, u32[]{:S(2)}, u32[]{:S(2)}) collective-permute-start(bf16[1,1,48,728]{3,2,1,0:T(8,128)(2,1)} %get-tuple-element.39), channel_id=1, source_target_pairs={{0,1},{1,2},{2,3},{3,4},{4,5},{5,6},{6,7},{8,9},{9,10},{10,11},{11... | collective-permute-start | bytes 209672 | tf_op jit(solution)/shard_map/ppermute | solution.py:15
  14.3 13.5 %collective-permute-start.1 = (bf16[1,1,48,728]{3,2,1,0:T(8,128)(2,1)S(1)}, bf16[1,1,48,728]{3,2,1,0:T(8,128)(2,1)S(1)}, u32[]{:S(2)}, u32[]{:S(2)}) collective-permute-start(bf16[1,1,48,728]{3,2,1,0:T(8,128)(2,1)S(1)} %get-tuple-element.40), channel_id=1, source_target_pairs={{1,0},{2,1},{3,2},{4,3},{5,4},{6,5},{7,6},{9,8},{10,9},{11,10},{12... | collective-permute-start | bytes 209672 | tf_op jit(solution)/shard_map/ppermute | solution.py:17
  17.6 3.1 copy-start.14
  28.7 0.8 copy-start.4
  30.9 38.0 %copy-start.11 = (f32[728]{0:T(1024)S(1)}, f32[728]{0:T(1024)}, u32[]{:S(2)}) copy-start(f32[728]{0:T(1024)} %param.14) | copy-start | bytes 8740
  30.9 38.1 %copy-start.12 = (f32[728]{0:T(1024)S(1)}, f32[728]{0:T(1024)}, u32[]{:S(2)}) copy-start(f32[728]{0:T(1024)} %param.15) | copy-start | bytes 8740
  71.6 1.0 copy-start.5
  72.6 2.1 copy-start.8
  384.1 40.9 %copy-start.9 = (bf16[288,728]{1,0:T(8,128)(2,1)S(1)}, bf16[288,728]{1,0:T(8,128)(2,1)}, u32[]{:S(2)}) copy-start(bf16[288,728]{1,0:T(8,128)(2,1)} %get-tuple-element.36) | copy-start | bytes 1257988
  416.2 10.7 %copy-start.10 = (f32[728,96]{0,1:T(8,128)}, f32[728,96]{0,1:T(8,128)S(1)}, u32[]{:S(2)}) copy-start(f32[728,96]{0,1:T(8,128)S(1)} %fusion) | copy-start | bytes 838660
  416.3 10.4 %collective-permute-start.2 = (bf16[1,1,48,728]{3,2,1,0:T(8,128)(2,1)S(1)}, bf16[1,1,48,728]{3,2,1,0:T(8,128)(2,1)S(1)}, u32[]{:S(2)}, u32[]{:S(2)}) collective-permute-start(bf16[1,1,48,728]{3,2,1,0:T(8,128)(2,1)S(1)} %get-tuple-element.37), channel_id=1, source_target_pairs={{0,1},{1,2},{2,3},{3,4},{4,5},{5,6},{6,7},{8,9},{9,10},{10,11},{11... | collective-permute-start | bytes 209672 | tf_op jit(solution)/shard_map/ppermute | solution.py:15
  418.4 8.4 %collective-permute-start.3 = (bf16[1,1,48,728]{3,2,1,0:T(8,128)(2,1)S(1)}, bf16[1,1,48,728]{3,2,1,0:T(8,128)(2,1)S(1)}, u32[]{:S(2)}, u32[]{:S(2)}) collective-permute-start(bf16[1,1,48,728]{3,2,1,0:T(8,128)(2,1)S(1)} %get-tuple-element.38), channel_id=1, source_target_pairs={{1,0},{2,1},{3,2},{4,3},{5,4},{6,5},{7,6},{9,8},{10,9},{11,10},{12... | collective-permute-start | bytes 209672 | tf_op jit(solution)/shard_map/ppermute | solution.py:17
  420.8 10.8 %collective-permute-start.4 = (f32[728,35]{0,1:T(8,128)}, f32[728,35]{0,1:T(8,128)S(1)}, u32[]{:S(2)}, u32[]{:S(2)}) collective-permute-start(f32[728,35]{0,1:T(8,128)} %slice.162), channel_id=1, source_target_pairs={{0,1},{1,2},{2,3},{3,4},{4,5},{5,6},{6,7},{8,9},{9,10},{10,11},{11... | collective-permute-start | bytes 305768
  428.5 7.2 copy-start.2
  428.5 7.2 copy-start.3
  428.5 7.2 copy-start.7
Sparse Core Ops, SparseCore 0:
  435.9 345.4 all-reduce.8
where the time goes:
time: 791 us; the launch traced here: 790 us
  blocking collectives  376 us (48%)
  waiting for transfers between devices  343 us (43%)
  local copies, waits for them, and re-layouts  22.6 us (3%)
  between operations  15.7 us (2%)
  other arithmetic  15.6 us (2%)
  starting transfers between devices  12.9 us (2%)
    psum x1, waiting for transfers between devices, local(): lax.psum((point_share, tap_share, gain_share, shift_share), 'dp')  343 us
    psum x1, blocking collectives, local(): lax.psum((point_share, tap_share, gain_share, shift_share), 'dp')  287 us
    unnamed x2, blocking collectives  52.6 us
    psum x2, blocking collectives, slab_totals(): return lax.psum((first, second), 'slab')  36.4 us
  transfers between devices with their start and end apart: 6, of which 1 were waited for; matrix products, arithmetic and copies ran while one was open for 3% of the time, Pallas kernels for 0%

commit v1 on v0

v1 whole, which is shorter than its diff:
```python
import functools

import jax
import jax.numpy as jnp
from jax import lax
from jax.experimental import pallas as pl
from jax.experimental.pallas import tpu as pltpu
from jax.sharding import PartitionSpec as P

MESH = pl.DeviceIdType.MESH
F32 = jnp.float32
BF16 = jnp.bfloat16

CH = 728
CP = 768
CB = CP // 128
WIDTH = 48
ROWS = 6
PIX = WIDTH * 8
GROUP = 16 * CH // 128
NZ, NX, NC, NY = 16, 4, 2, 8
SHARE = CH // NY
HALF = 48
NH = NY * HALF
TILES = HALF // 8 * CB
TX = TILES // NX
RED = [NZ * i // TX for i in range(TX)]
COUNT = float(ROWS * WIDTH * NY)
BATCH = float(NZ * NX * NC)


def lanes(i):
    return slice(128 * i, 128 * (i + 1))


def kernel(
    x_ref, u_ref, lab_ref, cw_ref, dk_ref, pw_ref, gain_ref, shift_ref,
    out_ref, gin_ref, gpw_ref, gdw_ref, gg_ref, gs_ref,
    X, A, U, PJ, D, GP, GD, WP, ST, SEL, RR, RS, GS, GR, H, RF, RB, VX, VZ, C, CM,
    HS, HR, BS, BR, STAT, VEC, RRECV,
    h_send, h_recv, b_send, b_recv, s_send, s_recv, g_send, g_recv,
    f_send, f_recv, k_send, k_recv, x_send, x_recv, z_send, z_recv,
    a_send, a_recv, ax_send, ax_recv, ac_send, ac_recv,
):
    dp = lax.axis_index("dp")
    y = lax.axis_index("slab")
    c = lax.rem(dp, NC)
    xx = lax.rem(dp // NC, NX)
    z = dp // (NC * NX)

    def at_y(k):
        return (dp, lax.rem(y + (k % NY), NY))

    def at_x(k):
        return ((z * NX + lax.rem(xx + (k % NX), NX)) * NC + c, y)

    def at_zz(zz):
        return ((zz * NX + xx) * NC + c, y)

    partner = ((z * NX + xx) * NC + (1 - c), y)

    def rcopy(src, dst, ss, rs, dev):
        return pltpu.make_async_remote_copy(
            src_ref=src, dst_ref=dst, send_sem=ss, recv_sem=rs,
            device_id=dev, device_id_type=MESH,
        )

    barrier = pltpu.get_barrier_semaphore()
    peers = [at_y(k) for k in range(1, NY)]
    peers += [at_x(k) for k in range(1, NX)]
    peers += [at_zz(lax.rem(z + k, NZ)) for k in range(1, NZ)]
    peers += [partner]
    for peer in peers:
        pl.semaphore_signal(barrier, inc=1, device_id=peer, device_id_type=MESH)

    lane_ok = lax.broadcasted_iota(jnp.int32, (ROWS, CP), 1) < CH

    def unflat(ref, base, k):
        off = CH * k
        first, sh = off // 128, off % 128
        nv = 6 if sh + CH <= CP else 7
        v = ref[:, pl.ds(pl.multiple_of(base + first * 128, 128), nv * 128)].astype(F32)
        if sh:
            v = pltpu.roll(v, nv * 128 - sh, axis=1)
        return jnp.where(lane_ok, v[:, :CP], 0.0)

    X[...] = jnp.zeros_like(X)

    def load_x(g, carry):
        for k in range(16):
            X[g * 16 + k, 0:ROWS, :] = unflat(x_ref, g * GROUP * 128, k)
        return carry

    lax.fori_loop(0, WIDTH // 16, load_x, 0)
    for side, row in ((0, 0), (1, ROWS - 1)):
        HS[side] = X[:, row, :].astype(BF16)

    lab = lab_ref[...]
    wt = jnp.where(
        lab == 0, cw_ref[0], jnp.where(lab == 1, cw_ref[1], jnp.where(lab == 2, cw_ref[2], 0.0))
    )
    U[...] = jnp.zeros_like(U)
    for w in range(WIDTH):
        U[w, 0:ROWS, :] = unflat(u_ref, (w // 16) * GROUP * 128, w % 16) * wt[:, w : w + 1]

    pl.semaphore_wait(barrier, len(peers))

    halo = [
        rcopy(HS.at[0], HR.at[0], h_send.at[0], h_recv.at[0], at_y(-1)),
        rcopy(HS.at[1], HR.at[1], h_send.at[1], h_recv.at[1], at_y(1)),
    ]
    for cp in halo:
        cp.start()

    WP[...] = jnp.zeros_like(WP)
    WP[0:CH, 0:CH] = pw_ref[...]
    row = lax.broadcasted_iota(jnp.int32, (NH, 128), 0)
    slab_of = jnp.zeros_like(row)
    for k in range(1, NY):
        slab_of = slab_of + jnp.where(row >= HALF * k, 1, 0)
    inner = row - HALF * slab_of
    lane = lax.broadcasted_iota(jnp.int32, (NH, 128), 1)
    for h in range(2):
        core = (1 - c) if h == 0 else c
        j = inner + HALF * core
        target = jnp.where(j < SHARE, SHARE * slab_of + j, -1)
        for b in range(CB):
            ST[h, :, lanes(b)] = jnp.where(lane + 128 * b == target, 1.0, 0.0).astype(BF16)

    for cp in halo:
        cp.wait()
    below = jnp.where(y < NY - 1, HR[0].astype(F32), 0.0)
    above = jnp.where(y > 0, HR[1].astype(F32), 0.0)
    X[:, ROWS, :] = below
    X[:, ROWS + 1, :] = above
    A[0] = jnp.zeros((8, CP), F32)
    A[WIDTH + 1] = jnp.zeros((8, CP), F32)
    A[1 : WIDTH + 1] = jnp.maximum(X[...], 0.0)

    own = lax.broadcasted_iota(jnp.int32, (8, 8, 128), 1) < ROWS
    own2 = lax.broadcasted_iota(jnp.int32, (8, 8, 128), 1) < ROWS

    for b in range(CB):
        k = [dk_ref[t : t + 1, lanes(b)].astype(F32) for t in range(9)]

        def conv(q, carry):
            a = A[pl.ds(q * 8, 10), :, lanes(b)]
            rows = [
                a[0:8] * k[3 * i] + a[1:9] * k[3 * i + 1] + a[2:10] * k[3 * i + 2]
                for i in range(3)
            ]
            d = pltpu.roll(rows[0], 1, axis=1) + rows[1] + pltpu.roll(rows[2], 7, axis=1)
            d = jnp.where(own, d, 0.0)
            D[pl.ds(pl.multiple_of(q * 64, 64), 64), lanes(b)] = d.reshape(64, 128).astype(BF16)
            return carry

        lax.fori_loop(0, WIDTH // 8, conv, 0)

    for nb in range(3):
        cols = slice(256 * nb, 256 * (nb + 1))
        PJ[:, :, cols] = jnp.dot(
            D[...], WP[:, cols], preferred_element_type=F32
        ).reshape(WIDTH, 8, 256)

    n_local = float(ROWS * WIDTH)
    for b in range(CB):
        s = jnp.zeros((8, 128), F32)
        g = jnp.zeros((8, 128), F32)
        for q in range(WIDTH // 8):
            s = s + jnp.sum(PJ[8 * q : 8 * q + 8, :, lanes(b)], axis=0)
            g = g + jnp.sum(U[8 * q : 8 * q + 8, :, lanes(b)], axis=0)
        s = jnp.sum(s, axis=0, keepdims=True)
        g = jnp.sum(g, axis=0, keepdims=True)
        mu = s * (1.0 / n_local)
        m2 = jnp.zeros((8, 128), F32)
        cr = jnp.zeros((8, 128), F32)
        for q in range(WIDTH // 8):
            dev = jnp.where(own2, PJ[8 * q : 8 * q + 8, :, lanes(b)] - mu, 0.0)
            m2 = m2 + jnp.sum(dev * dev, axis=0)
            cr = cr + jnp.sum(dev * U[8 * q : 8 * q + 8, :, lanes(b)], axis=0)
        m2 = jnp.sum(m2, axis=0, keepdims=True)
        cr = jnp.sum(cr, axis=0, keepdims=True)
        STAT[y, :, lanes(b)] = jnp.concatenate([s, g, m2, cr], axis=0)
    stat = []
    for k in range(1, NY):
        cp = rcopy(STAT.at[y], STAT.at[y], s_send.at[k - 1], s_recv.at[k - 1], at_y(k))
        cp.start()
        stat.append(cp)
    for cp in stat:
        cp.wait()

    total = STAT[0, 0:2, :]
    for i in range(1, NY):
        total = total + STAT[i, 0:2, :]
    center = total[0:1] * (1.0 / COUNT)
    shift_part = total[1:2]
    square = jnp.zeros((1, CP), F32)
    cross = jnp.zeros((1, CP), F32)
    for i in range(NY):
        off = STAT[i, 0:1, :] * (1.0 / n_local) - center
        square = square + STAT[i, 2:3, :] + n_local * off * off
        cross = cross + STAT[i, 3:4, :] + off * STAT[i, 1:2, :]
    inverse = lax.rsqrt(square * (1.0 / COUNT) + 1e-05)
    gain_part = cross * inverse
    mine = STAT[y]
    off = mine[0:1] * (1.0 / n_local) - center
    gain_local = (mine[3:4] + off * mine[1:2]) * inverse
    shift_local = mine[1:2]
    gain = gain_ref[...]
    VEC[0:1] = center
    VEC[1:2] = inverse
    VEC[2:3] = gain
    VEC[3:4] = shift_ref[...]
    VEC[4:5] = gain * inverse
    VEC[5:6] = shift_part * (1.0 / COUNT)
    VEC[6:7] = gain_part * (1.0 / COUNT)

    for b in range(CB):
        v = [VEC[i : i + 1, lanes(b)] for i in range(7)]

        def proj(q, carry):
            rows = pl.ds(q * 8, 8)
            normed = (PJ[rows, :, lanes(b)] - v[0]) * v[1]
            gp = v[4] * (U[rows, :, lanes(b)] - v[5] - normed * v[6])
            gp = jnp.where(own, gp, 0.0)
            GP[pl.ds(pl.multiple_of(q * 64, 64), 64), lanes(b)] = gp.reshape(64, 128).astype(BF16)
            return carry

        lax.fori_loop(0, WIDTH // 8, proj, 0)

    NT = (((1,), (1,)), ((), ()))

    def weight_half(h, dst):
        SEL[...] = lax.dot_general(
            ST[h], GP[...], NT, preferred_element_type=F32
        ).astype(BF16)
        for nb in range(3):
            part = jnp.dot(
                SEL[...], D[:, 256 * nb : 256 * nb + 256], preferred_element_type=F32
            )
            for s in range(NY):
                for i in range(HALF // 8):
                    for j in range(2):
                        r = HALF * s + 8 * i
                        dst[s, i * CB + 2 * nb + j] = part[r : r + 8, lanes(j)]

    weight_half(0, GS)
    g_copy = rcopy(GS, GR, g_send.at[0], g_recv.at[0], partner)
    g_copy.start()

    GD[0] = jnp.zeros((8, CP), F32)
    GD[WIDTH + 1] = jnp.zeros((8, CP), F32)
    for nb in range(3):
        rows = slice(256 * nb, 256 * (nb + 1))
        gd = lax.dot_general(GP[...], WP[rows, :], NT, preferred_element_type=F32)
        GD[1 : WIDTH + 1, :, rows] = gd.astype(BF16).astype(F32).reshape(WIDTH, 8, 256)
    BS[0] = GD[1 : WIDTH + 1, 0, :].astype(BF16)
    BS[1] = GD[1 : WIDTH + 1, ROWS - 1, :].astype(BF16)
    back = [
        rcopy(BS.at[0], BR.at[0], b_send.at[0], b_recv.at[0], at_y(-1)),
        rcopy(BS.at[1], BR.at[1], b_send.at[1], b_recv.at[1], at_y(1)),
    ]
    for cp in back:
        cp.start()

    RR[...] = jnp.zeros_like(RR)
    for b in range(CB):

        def tap(q, acc):
            a = A[pl.ds(q * 8, 10), :, lanes(b)]
            gd = GD[pl.ds(q * 8 + 1, 8), :, lanes(b)]
            shifted = [pltpu.roll(gd, 7, axis=1), gd, pltpu.roll(gd, 1, axis=1)]
            return tuple(
                acc[3 * i + j] + jnp.sum(a[j : j + 8] * shifted[i], axis=0)
                for i in range(3)
                for j in range(3)
            )

        acc = lax.fori_loop(
            0, WIDTH // 8, tap, tuple(jnp.zeros((8, 128), F32) for _ in range(9))
        )
        for t in range(9):
            RR[t : t + 1, lanes(b)] = jnp.sum(acc[t], axis=0, keepdims=True)
    RR[9:10] = gain_local
    RR[10:11] = shift_local
    r_copy = rcopy(RR, RRECV, g_send.at[1], g_recv.at[1], partner)
    r_copy.start()

    weight_half(1, H)
    RS[...] = jnp.zeros_like(RS)
    g_copy.wait()
    r_copy.wait()
    RS[CH - 640 : CH - 640 + 16] = RR[...] + RRECV[...]
    rest = RS[...]
    extra = jnp.zeros((NH, 128), F32)
    for _ in range(3):
        part = rest.astype(BF16)
        rest = rest - part.astype(F32)
        extra = extra + lax.dot_general(ST[1], part, NT, preferred_element_type=F32)
    for s in range(NY):
        H[s] = H[s] + GR[s]
        for i in range(HALF // 8):
            r = HALF * s + 8 * i
            H[s, i * CB + CB - 1] = H[s, i * CB + CB - 1] + extra[r : r + 8]

    def piece(h):
        return pl.ds(TX * h, TX)

    def down(t, h):
        return rcopy(
            H.at[lax.rem(y + NY // 2 - t, NY), piece(h)] if t == 0 or (t == 1 and h >= 2)
            else RF.at[t - 1, piece(h)],
            RF.at[t, piece(h)], f_send.at[t, h], f_recv.at[t, h], at_y(1),
        )

    def up(t, h):
        return rcopy(
            H.at[lax.rem(y + NY // 2 + t, NY), piece(h)] if t == 0 or (t == 1 and h < 2)
            else RB.at[t - 1, piece(h)],
            RB.at[t, piece(h)], k_send.at[t, h], k_recv.at[t, h], at_y(-1),
        )

    def forward(t):
        for h in range(NX):
            if t == 0:
                (down if h < 2 else up)(0, h).start()
                continue
            if t > 1 or h < 2:
                down(t - 1, h).wait_recv()
                RF[t - 1, piece(h)] = (
                    RF[t - 1, piece(h)] + H[lax.rem(y + NY // 2 - t, NY), piece(h)]
                )
            down(t, h).start()
            if t > 1 or h >= 2:
                up(t - 1, h).wait_recv()
                RB[t - 1, piece(h)] = (
                    RB[t - 1, piece(h)] + H[lax.rem(y + NY // 2 + t, NY), piece(h)]
                )
            up(t, h).start()

    forward(0)

    def reflat(ref, column):
        first_lane = lax.broadcasted_iota(jnp.int32, (8, 128), 1)

        def body(g, carry):
            tail = jnp.zeros((8, 128), F32)
            for k in range(16):
                off = CH * k
                first, sh = off // 128, off % 128
                v = column(g * 16 + k)
                if sh:
                    v = pltpu.roll(
                        jnp.concatenate([v, jnp.zeros((8, 128), F32)], axis=1), sh, axis=1
                    )
                    head = jnp.where(first_lane < sh, tail, v[:, :128])
                    v = jnp.concatenate([head, v[:, 128:]], axis=1)
                full = (sh + CH) // 128
                start = pl.multiple_of((g * GROUP + first) * 128, 128)
                ref[:, pl.ds(start, full * 128)] = v[0:ROWS, : full * 128].astype(BF16)
                if k < 15:
                    tail = v[:, full * 128 : full * 128 + 128]
            return carry

        lax.fori_loop(0, WIDTH // 16, body, 0)

    def out_column(w):
        normed = (PJ[w] - VEC[0:1]) * VEC[1:2]
        return X[w] + VEC[2:3] * normed + VEC[3:4]

    reflat(out_ref, out_column)
    forward(1)

    for cp in back:
        cp.wait()
    GD[1 : WIDTH + 1, ROWS, :] = jnp.where(y < NY - 1, BR[0].astype(F32), 0.0)
    GD[1 : WIDTH + 1, ROWS + 1, :] = jnp.where(y > 0, BR[1].astype(F32), 0.0)
    for b in range(CB):
        k = [dk_ref[t : t + 1, lanes(b)].astype(F32) for t in range(9)]

        def conv_t(q, carry):
            a = GD[pl.ds(q * 8, 10), :, lanes(b)]
            rows = [
                a[2:10] * k[3 * i] + a[1:9] * k[3 * i + 1] + a[0:8] * k[3 * i + 2]
                for i in range(3)
            ]
            d = pltpu.roll(rows[0], 7, axis=1) + rows[1] + pltpu.roll(rows[2], 1, axis=1)
            cols = pl.ds(q * 8, 8)
            PJ[cols, :, lanes(b)] = U[cols, :, lanes(b)] + jnp.where(
                X[cols, :, lanes(b)] > 0.0, d, 0.0
            )
            return carry

        lax.fori_loop(0, WIDTH // 8, conv_t, 0)
    forward(2)
    reflat(gin_ref, lambda w: PJ[w])
    forward(3)

    for h in range(NX):
        down(3, h).wait_recv()
        up(3, h).wait_recv()
        H[y, piece(h)] = H[y, piece(h)] + RF[3, piece(h)] + RB[3, piece(h)]
        d = lax.rem(h - xx + NX, NX)

        @pl.when(d != 0)
        def _():
            rcopy(
                H.at[y, piece(h)], VX.at[d - 1], x_send.at[d - 1], x_recv.at[d - 1],
                ((z * NX + h) * NC + c, y),
            ).start()

    v = H[y, pl.ds(pl.multiple_of(TX * xx, TX), TX)]
    for k in range(1, NX):
        cp = rcopy(VX.at[k - 1], VX.at[k - 1], x_send.at[k - 1], x_recv.at[k - 1], at_x(k))
        cp.wait_recv()
        v = v + VX[k - 1]
    GS[0, 0:TX] = v

    mine_i = (TX * z + NZ - 1) // NZ
    is_red = jnp.logical_and(mine_i < TX, (NZ * mine_i) // TX == z)

    def to_red(i):
        d = lax.rem(z - RED[i] + NZ, NZ)
        return rcopy(
            GS.at[0, i], VZ.at[d - 1], z_send.at[i], z_recv.at[d - 1], at_zz(RED[i])
        )

    for i in range(TX):

        @pl.when(z != RED[i])
        def _():
            to_red(i).start()

    @pl.when(is_red)
    def _():
        s = GS[0, mine_i]
        for d in range(1, NZ):
            rcopy(
                VZ.at[d - 1], VZ.at[d - 1], z_send.at[0], z_recv.at[d - 1],
                at_zz(lax.rem(z + d, NZ)),
            ).wait_recv()
            s = s + VZ[d - 1]
        C[c, TX * xx + mine_i] = s * (1.0 / BATCH)
        for d in range(1, NZ):
            tile = C.at[c, TX * xx + mine_i]
            rcopy(
                tile, tile, a_send.at[d - 1], a_recv.at[mine_i], at_zz(lax.rem(z + d, NZ))
            ).start()

    for i in range(TX):

        @pl.when(z != RED[i])
        def _():
            tile = C.at[c, TX * xx + i]
            rcopy(tile, tile, a_send.at[0], a_recv.at[i], at_zz(RED[i])).wait_recv()

    def part(core, x0):
        return C.at[core, pl.ds(pl.multiple_of(TX * x0, TX), TX)]

    for k in range(1, NX):
        rcopy(part(c, xx), part(c, xx), ax_send.at[k - 1], ax_recv.at[k - 1], at_x(k)).start()
    rcopy(part(c, xx), part(c, xx), ac_send.at[0], ac_recv.at[0], partner).start()
    for k in range(1, NX):
        x0 = lax.rem(xx - k + NX, NX)
        rcopy(part(c, x0), part(c, x0), ax_send.at[k - 1], ax_recv.at[k - 1], at_x(k)).wait_recv()
        rcopy(part(c, x0), part(c, x0), ac_send.at[k], ac_recv.at[k], partner).start()
    for k in range(NX):
        x0 = lax.rem(xx - k + NX, NX)
        cp = rcopy(part(1 - c, x0), part(1 - c, x0), ac_send.at[k], ac_recv.at[k], partner)
        cp.wait_recv()

    CM[...] = jnp.zeros_like(CM)
    for core in range(NC):
        for i in range(HALF // 8):
            for j in range(CB):
                r = core * HALF + 8 * i
                CM[r : r + 8, lanes(j)] = C[core, i * CB + j]
    for j in range(CB):
        t = CM[:, lanes(j)].T
        if j < CB - 1:
            gpw_ref[lanes(j), :] = t[:, :SHARE]
        else:
            cut = CH - 128 * j
            gpw_ref[128 * j : CH, :] = t[:cut, :SHARE]
            gdw_ref[...] = t[cut : cut + 9, :SHARE]
            gg_ref[...] = t[cut + 9 : cut + 10, :SHARE]
            gs_ref[...] = t[cut + 10 : cut + 11, :SHARE]

    for t in range(4):
        for h in range(NX):
            if t > 0 or h < 2:
                down(t, h).wait_send()
            if t > 0 or h >= 2:
                up(t, h).wait_send()
    for k in range(1, NX):
        rcopy(VX.at[k - 1], VX.at[k - 1], x_send.at[k - 1], x_recv.at[k - 1], at_x(k)).wait_send()
    for i in range(TX):

        @pl.when(z != RED[i])
        def _():
            to_red(i).wait_send()

    @pl.when(is_red)
    def _():
        for d in range(1, NZ):
            tile = C.at[c, TX * xx + mine_i]
            rcopy(
                tile, tile, a_send.at[d - 1], a_recv.at[mine_i], at_zz(lax.rem(z + d, NZ))
            ).wait_send()

    for k in range(1, NX):
        rcopy(part(c, xx), part(c, xx), ax_send.at[k - 1], ax_recv.at[k - 1], at_x(k)).wait_send()
    for k in range(NX):
        x0 = lax.rem(xx - k + NX, NX)
        rcopy(part(c, x0), part(c, x0), ac_send.at[k], ac_recv.at[k], partner).wait_send()


def local(inputs, upstream, labels, class_weights, depth_kernel, point_weight, gain, shift):
    vm = pl.BlockSpec(memory_space=pltpu.VMEM)
    dma = pltpu.SemaphoreType.DMA
    wide = (1, CP)

    def pad_row(row):
        return jnp.pad(row[None, :], ((0, 0), (0, CP - CH)))

    outs = pl.pallas_call(
        kernel,
        out_shape=(
            jax.ShapeDtypeStruct((ROWS, WIDTH * CH), BF16),
            jax.ShapeDtypeStruct((ROWS, WIDTH * CH), BF16),
            jax.ShapeDtypeStruct((CH, SHARE), F32),
            jax.ShapeDtypeStruct((9, SHARE), F32),
            jax.ShapeDtypeStruct((1, SHARE), F32),
            jax.ShapeDtypeStruct((1, SHARE), F32),
        ),
        in_specs=[vm, vm, vm, pl.BlockSpec(memory_space=pltpu.SMEM), vm, vm, vm, vm],
        out_specs=(vm,) * 6,
        scratch_shapes=[
            pltpu.VMEM((WIDTH, 8, CP), F32),
            pltpu.VMEM((WIDTH + 2, 8, CP), F32),
            pltpu.VMEM((WIDTH, 8, CP), F32),
            pltpu.VMEM((WIDTH, 8, CP), F32),
            pltpu.VMEM((PIX, CP), BF16),
            pltpu.VMEM((PIX, CP), BF16),
            pltpu.VMEM((WIDTH + 2, 8, CP), F32),
            pltpu.VMEM((CP, CP), BF16),
            pltpu.VMEM((2, NH, CP), BF16),
            pltpu.VMEM((NH, PIX), BF16),
            pltpu.VMEM((16, CP), F32),
            pltpu.VMEM((128, CP), F32),
            pltpu.VMEM((NY, TILES, 8, 128), F32),
            pltpu.VMEM((NY, TILES, 8, 128), F32),
            pltpu.VMEM((NY, TILES, 8, 128), F32),
            pltpu.VMEM((4, TILES, 8, 128), F32),
            pltpu.VMEM((4, TILES, 8, 128), F32),
            pltpu.VMEM((NX - 1, TX, 8, 128), F32),
            pltpu.VMEM((NZ - 1, 8, 128), F32),
            pltpu.VMEM((NC, TILES, 8, 128), F32),
            pltpu.VMEM((128, CP), F32),
            pltpu.VMEM((2, WIDTH, CP), BF16),
            pltpu.VMEM((2, WIDTH, CP), BF16),
            pltpu.VMEM((2, WIDTH, CP), BF16),
            pltpu.VMEM((2, WIDTH, CP), BF16),
            pltpu.VMEM((NY, 4, CP), F32),
            pltpu.VMEM((8, CP), F32),
            pltpu.VMEM((16, CP), F32),
            dma((2,)), dma((2,)), dma((2,)), dma((2,)),
            dma((NY - 1,)), dma((NY - 1,)), dma((2,)), dma((2,)),
            dma((4, NX)), dma((4, NX)), dma((4, NX)), dma((4, NX)),
            dma((NX - 1,)), dma((NX - 1,)), dma((TX,)), dma((NZ - 1,)),
            dma((NZ - 1,)), dma((TX,)), dma((NX - 1,)), dma((NX - 1,)),
            dma((NX,)), dma((NX,)),
        ],
        compiler_params=pltpu.CompilerParams(
            collective_id=0, has_side_effects=True, vmem_limit_bytes=48 * 1024 * 1024
        ),
    )(
        inputs.reshape(ROWS, WIDTH * CH),
        upstream.reshape(ROWS, WIDTH * CH),
        labels.reshape(ROWS, WIDTH),
        class_weights,
        jnp.pad(depth_kernel, ((0, 0), (0, CP - CH))),
        point_weight,
        pad_row(gain),
        pad_row(shift),
    )
    block_out, grad_in, gpw, gdw, gg, gs = outs
    return (
        block_out.reshape(1, ROWS, WIDTH * CH),
        grad_in.reshape(1, ROWS, WIDTH * CH),
        gpw,
        gdw,
        gg.reshape(SHARE),
        gs.reshape(SHARE),
    )


def solution(mesh):
    return jax.shard_map(
        local,
        mesh=mesh,
        in_specs=(
            P("dp", "slab", None),
            P("dp", "slab", None),
            P("dp", "slab", None),
            P(), P(), P(), P(), P(),
        ),
        out_specs=(
            P("dp", "slab", None),
            P("dp", "slab", None),
            P(None, "slab"),
            P(None, "slab"),
            P("slab"),
            P("slab"),
        ),
        check_vma=False,
    )
```

time: 791 us -> 94.1 us (0.12)
  blocking collectives: 376 us -> 0 us
  waiting for transfers between devices: 343 us -> 0 us
  Pallas kernels: 0 us -> 82.1 us
  other arithmetic: 15.6 us -> 0 us
  between operations: 15.7 us -> 0.65 us
  starting transfers between devices: 12.9 us -> 0 us
  local copies, waits for them, and re-layouts: 22.6 us -> 11 us
    psum x1 -> x0, waiting for transfers between devices: 343 us -> none  [local(): lax.psum((point_share, tap_share, gain_share, shift_share), 'dp')]
    psum x3 -> x0, blocking collectives: 323 us -> none  [the longest x1 287 us: local(): lax.psum((point_share, tap_share, gain_share, shift_share), 'dp')]
    pallas_call x0 -> x1, Pallas kernels: none -> 82.1 us  [local(): pl.pallas_call(kernel, out_shape=(jax.ShapeDtypeStruct((ROWS, WIDTH * CH)...]
    unnamed x2 -> x0, blocking collectives: 52.6 us -> none
    ppermute x4 -> x0, starting transfers between devices: 8.67 us -> none  [the longest x2 6.09 us: padded_2(): lax.ppermute(tail, axis, [(i, (i + 1) % count) for i in range(ends)])]
  transfers between devices with their start and end apart: 6 -> 0, of which waited for: 1 -> 0; matrix products, arithmetic and copies ran while one was open for 3% -> 0% of each run, Pallas kernels for 0% -> 0%
where the time goes in v1:
time: 94.1 us; the launch traced here: 93.7 us
  Pallas kernels  82.1 us (87%)
  local copies, waits for them, and re-layouts  11 us (12%)
    pallas_call x1, Pallas kernels, local(): pl.pallas_call(kernel, out_shape=(jax.ShapeDtypeStruct((ROWS, WIDTH * CH)...  82.1 us
    unnamed x15, local copies, waits for them, and re-layouts  8.81 us

profile of v1, /device:TPU:1, one launch (start us, length us, event | category | flops | bytes accessed | tf_op | source)
XLA Modules:
  0.0 93.7 jit_solution(18175128461788927921)
XLA Ops:
  0.6 0.7 broadcast_in_dim.6
  1.3 0.7 broadcast_in_dim.7
  2.0 0.7 copy.17
  2.7 0.7 pad.11.dk_ref
  3.5 0.0 copy-start
  3.5 1.2 %copy-done = bf16[728,728]{1,0:T(8,128)(2,1)S(1)} copy-done((bf16[728,728]{1,0:T(8,128)(2,1)S(1)}, bf16[728,728]{1,0:T(8,128)(2,1)}, u32[]{:S(2)}) %copy-start) | copy-done | bytes 1059992
  4.7 0.0 copy-start.1
  4.7 1.1 %copy-done.1 = bf16[1,6,34944]{2,1,0:T(8,128)(2,1)S(1)} copy-done((bf16[1,6,34944]{2,1,0:T(8,128)(2,1)S(1)}, bf16[1,6,34944]{2,1,0:T(8,128)(2,1)}, u32[]{:S(2)}) %copy-start.1) | copy-done | bytes 419352
  5.8 0.0 copy-start.2
  5.8 1.1 %copy-done.2 = bf16[1,6,34944]{2,1,0:T(8,128)(2,1)S(1)} copy-done((bf16[1,6,34944]{2,1,0:T(8,128)(2,1)S(1)}, bf16[1,6,34944]{2,1,0:T(8,128)(2,1)}, u32[]{:S(2)}) %copy-start.2) | copy-done | bytes 419352
  6.8 0.0 copy-start.3
  6.8 0.7 copy-done.3
  7.5 82.1 %shard_map.127 = (bf16[6,34944]{1,0:T(8,128)(2,1)S(1)}, bf16[6,34944]{1,0:T(8,128)(2,1)S(1)}, f32[728,91]{1,0:T(8,128)S(1)}, f32[9,91]{1,0:T(8,128)S(1)}, f32[1,91]{1,0:T(1,128)S(1)}, /*index=5*/f32[1,91]{1,0:T(1,128)S(1)}) custom-call(bf16[6,34944]{1,0:T(8,128)(2,1)S(1)} %bitcast.9, bf16[6,34944]{1,0:T(8,128)(2,1)S(1)} %bitcast.10, s32[6,48]{1,0:T(8,128)S(1)} %bitcast.13, ...), custom_call_target="tpu_custom_call" | custom-call | tf_op jit(solution)/shard_map/pallas_call | solution.py:526
  89.5 0.9 copy.14
  90.4 0.8 copy.23
  91.2 0.8 copy.24
  92.0 0.6 copy.25
  92.6 0.5 copy.26
  93.1 0.5 copy.27
  (2 shorter events, 0.0 us)
Async XLA Ops:
  3.5 1.2 %copy-start = (bf16[728,728]{1,0:T(8,128)(2,1)S(1)}, bf16[728,728]{1,0:T(8,128)(2,1)}, u32[]{:S(2)}) copy-start(bf16[728,728]{1,0:T(8,128)(2,1)} %pw_ref.1) | copy-start | bytes 3179908
  4.7 1.1 %copy-start.1 = (bf16[1,6,34944]{2,1,0:T(8,128)(2,1)S(1)}, bf16[1,6,34944]{2,1,0:T(8,128)(2,1)}, u32[]{:S(2)}) copy-start(bf16[1,6,34944]{2,1,0:T(8,128)(2,1)} %param.8) | copy-start | bytes 1257988
  5.8 1.1 %copy-start.2 = (bf16[1,6,34944]{2,1,0:T(8,128)(2,1)S(1)}, bf16[1,6,34944]{2,1,0:T(8,128)(2,1)}, u32[]{:S(2)}) copy-start(bf16[1,6,34944]{2,1,0:T(8,128)(2,1)} %param.9) | copy-start | bytes 1257988
  6.8 0.7 copy-start.3

commit v2 on v1

--- a/solution.py
+++ b/solution.py
@@ -34,8 +34,9 @@
 
 
 def kernel(
-    x_ref, u_ref, lab_ref, cw_ref, dk_ref, pw_ref, gain_ref, shift_ref,
+    x_hbm, u_hbm, lab_hbm, cw_hbm, dk_hbm, pw_hbm, gain_hbm, shift_hbm,
     out_ref, gin_ref, gpw_ref, gdw_ref, gg_ref, gs_ref,
+    x_ref, u_ref, lab_ref, cw_ref, dk_ref, pw_ref, gain_ref, shift_ref, in_sem, DK,
     X, A, U, PJ, D, GP, GD, WP, ST, SEL, RR, RS, GS, GR, H, RF, RB, VX, VZ, C, CM,
     HS, HR, BS, BR, STAT, VEC, RRECV,
     h_send, h_recv, b_send, b_recv, s_send, s_recv, g_send, g_recv,
@@ -65,6 +66,15 @@
             device_id=dev, device_id_type=MESH,
         )
 
+    loads = [
+        pltpu.make_async_copy(src, dst, in_sem.at[i])
+        for i, (src, dst) in enumerate((
+            (x_hbm, x_ref), (u_hbm, u_ref), (lab_hbm, lab_ref), (cw_hbm, cw_ref),
+            (dk_hbm, dk_ref), (pw_hbm, pw_ref), (gain_hbm, gain_ref), (shift_hbm, shift_ref),
+        ))
+    ]
+    for cp in loads:
+        cp.start()
     barrier = pltpu.get_barrier_semaphore()
     peers = [at_y(k) for k in range(1, NY)]
     peers += [at_x(k) for k in range(1, NX)]
@@ -85,6 +95,10 @@
         return jnp.where(lane_ok, v[:, :CP], 0.0)
 
     X[...] = jnp.zeros_like(X)
+    U[...] = jnp.zeros_like(U)
+    WP[...] = jnp.zeros_like(WP)
+    DK[...] = jnp.zeros_like(DK)
+    loads[0].wait()
 
     def load_x(g, carry):
         for k in range(16):
@@ -95,11 +109,13 @@
     for side, row in ((0, 0), (1, ROWS - 1)):
         HS[side] = X[:, row, :].astype(BF16)
 
-    lab = lab_ref[...]
+    for cp in loads[1:]:
+        cp.wait()
+    lab = jnp.concatenate([lab_ref[r] for r in range(ROWS)], axis=0)
+    DK[0:9, 0:CH] = dk_ref[...].astype(F32)
     wt = jnp.where(
         lab == 0, cw_ref[0], jnp.where(lab == 1, cw_ref[1], jnp.where(lab == 2, cw_ref[2], 0.0))
     )
-    U[...] = jnp.zeros_like(U)
     for w in range(WIDTH):
         U[w, 0:ROWS, :] = unflat(u_ref, (w // 16) * GROUP * 128, w % 16) * wt[:, w : w + 1]
 
@@ -112,7 +128,6 @@
     for cp in halo:
         cp.start()
 
-    WP[...] = jnp.zeros_like(WP)
     WP[0:CH, 0:CH] = pw_ref[...]
     row = lax.broadcasted_iota(jnp.int32, (NH, 128), 0)
     slab_of = jnp.zeros_like(row)
@@ -141,7 +156,7 @@
     own2 = lax.broadcasted_iota(jnp.int32, (8, 8, 128), 1) < ROWS
 
     for b in range(CB):
-        k = [dk_ref[t : t + 1, lanes(b)].astype(F32) for t in range(9)]
+        k = [DK[t : t + 1, lanes(b)] for t in range(9)]
 
         def conv(q, carry):
             a = A[pl.ds(q * 8, 10), :, lanes(b)]
@@ -206,11 +221,12 @@
     off = mine[0:1] * (1.0 / n_local) - center
     gain_local = (mine[3:4] + off * mine[1:2]) * inverse
     shift_local = mine[1:2]
-    gain = gain_ref[...]
+    pad = jnp.zeros((1, CP - CH), F32)
+    gain = jnp.concatenate([gain_ref[...].reshape(1, CH), pad], axis=1)
     VEC[0:1] = center
     VEC[1:2] = inverse
     VEC[2:3] = gain
-    VEC[3:4] = shift_ref[...]
+    VEC[3:4] = jnp.concatenate([shift_ref[...].reshape(1, CH), pad], axis=1)
     VEC[4:5] = gain * inverse
     VEC[5:6] = shift_part * (1.0 / COUNT)
     VEC[6:7] = gain_part * (1.0 / COUNT)
@@ -376,7 +392,7 @@
     GD[1 : WIDTH + 1, ROWS, :] = jnp.where(y < NY - 1, BR[0].astype(F32), 0.0)
     GD[1 : WIDTH + 1, ROWS + 1, :] = jnp.where(y > 0, BR[1].astype(F32), 0.0)
     for b in range(CB):
-        k = [dk_ref[t : t + 1, lanes(b)].astype(F32) for t in range(9)]
+        k = [DK[t : t + 1, lanes(b)] for t in range(9)]
 
         def conv_t(q, carry):
             a = GD[pl.ds(q * 8, 10), :, lanes(b)]
@@ -475,16 +491,12 @@
             for j in range(CB):
                 r = core * HALF + 8 * i
                 CM[r : r + 8, lanes(j)] = C[core, i * CB + j]
-    for j in range(CB):
-        t = CM[:, lanes(j)].T
-        if j < CB - 1:
-            gpw_ref[lanes(j), :] = t[:, :SHARE]
-        else:
-            cut = CH - 128 * j
-            gpw_ref[128 * j : CH, :] = t[:cut, :SHARE]
-            gdw_ref[...] = t[cut : cut + 9, :SHARE]
-            gg_ref[...] = t[cut + 9 : cut + 10, :SHARE]
-            gs_ref[...] = t[cut + 10 : cut + 11, :SHARE]
+    gpw_ref[...] = CM[0:SHARE, 0:CH]
+    cut = CH - 128 * (CB - 1)
+    t = CM[:, lanes(CB - 1)].T
+    gdw_ref[...] = t[cut : cut + 9, :SHARE]
+    gg_ref[...] = t[cut + 9 : cut + 10, :SHARE]
+    gs_ref[...] = t[cut + 10 : cut + 11, :SHARE]
 
     for t in range(4):
         for h in range(NX):
@@ -515,27 +527,43 @@
         rcopy(part(c, x0), part(c, x0), ac_send.at[k], ac_recv.at[k], partner).wait_send()
 
 
+def store(*refs):
+    sem = refs[12]
+    copies = [pltpu.make_async_copy(refs[i], refs[6 + i], sem.at[i]) for i in range(6)]
+    for cp in copies:
+        cp.start()
+    for cp in copies:
+        cp.wait()
+
+
 def local(inputs, upstream, labels, class_weights, depth_kernel, point_weight, gain, shift):
     vm = pl.BlockSpec(memory_space=pltpu.VMEM)
     dma = pltpu.SemaphoreType.DMA
-    wide = (1, CP)
-
-    def pad_row(row):
-        return jnp.pad(row[None, :], ((0, 0), (0, CP - CH)))
-
-    outs = pl.pallas_call(
-        kernel,
-        out_shape=(
+    hbm = pl.BlockSpec(memory_space=pltpu.HBM)
+    shapes = (
             jax.ShapeDtypeStruct((ROWS, WIDTH * CH), BF16),
             jax.ShapeDtypeStruct((ROWS, WIDTH * CH), BF16),
-            jax.ShapeDtypeStruct((CH, SHARE), F32),
+            jax.ShapeDtypeStruct((SHARE, CH), F32),
             jax.ShapeDtypeStruct((9, SHARE), F32),
             jax.ShapeDtypeStruct((1, SHARE), F32),
             jax.ShapeDtypeStruct((1, SHARE), F32),
-        ),
-        in_specs=[vm, vm, vm, pl.BlockSpec(memory_space=pltpu.SMEM), vm, vm, vm, vm],
+    )
+    outs = pl.pallas_call(
+        kernel,
+        out_shape=shapes,
+        in_specs=[hbm] * 8,
         out_specs=(vm,) * 6,
         scratch_shapes=[
+            pltpu.VMEM((ROWS, WIDTH * CH), BF16),
+            pltpu.VMEM((ROWS, WIDTH * CH), BF16),
+            pltpu.VMEM((ROWS, 1, WIDTH), jnp.int32),
+            pltpu.SMEM((3,), F32),
+            pltpu.VMEM((9, CH), BF16),
+            pltpu.VMEM((CH, CH), BF16),
+            pltpu.VMEM((CH,), F32),
+            pltpu.VMEM((CH,), F32),
+            dma((8,)),
+            pltpu.VMEM((16, CP), F32),
             pltpu.VMEM((WIDTH, 8, CP), F32),
             pltpu.VMEM((WIDTH + 2, 8, CP), F32),
             pltpu.VMEM((WIDTH, 8, CP), F32),
@@ -575,20 +603,32 @@
             collective_id=0, has_side_effects=True, vmem_limit_bytes=48 * 1024 * 1024
         ),
     )(
-        inputs.reshape(ROWS, WIDTH * CH),
-        upstream.reshape(ROWS, WIDTH * CH),
-        labels.reshape(ROWS, WIDTH),
-        class_weights,
-        jnp.pad(depth_kernel, ((0, 0), (0, CP - CH))),
-        point_weight,
-        pad_row(gain),
-        pad_row(shift),
+        *(
+            pltpu.with_memory_space_constraint(a, pltpu.HBM)
+            for a in (
+                inputs.reshape(ROWS, WIDTH * CH),
+                upstream.reshape(ROWS, WIDTH * CH),
+                labels.reshape(ROWS, 1, WIDTH),
+                class_weights,
+                depth_kernel,
+                point_weight,
+                gain,
+                shift,
+            )
+        )
     )
+    outs = pl.pallas_call(
+        store,
+        out_shape=shapes,
+        in_specs=[vm] * 6,
+        out_specs=(hbm,) * 6,
+        scratch_shapes=[dma((6,))],
+    )(*(pltpu.with_memory_space_constraint(a, pltpu.VMEM) for a in outs))
     block_out, grad_in, gpw, gdw, gg, gs = outs
     return (
         block_out.reshape(1, ROWS, WIDTH * CH),
         grad_in.reshape(1, ROWS, WIDTH * CH),
-        gpw,
+        gpw.T,
         gdw,
         gg.reshape(SHARE),
         gs.reshape(SHARE),

time: 94.1 us -> 83.5 us (0.89)
  local copies, waits for them, and re-layouts: 11 us -> 0 us
    unnamed x15 -> x0, local copies, waits for them, and re-layouts: 8.81 us -> none
    broadcast_in_dim x2 -> x0, local copies, waits for them, and re-layouts: 1.38 us -> none  [pad_row(): return jnp.pad(row[None, :], ((0, 0), (0, CP - CH)))]
    pallas_call x1 -> x2, Pallas kernels: 82.1 us -> 82.7 us  [the longest x1 81.5 us: local(): pl.pallas_call(kernel, out_shape=shapes, in_specs=[hbm] * 8, out_specs=(v...]
where the time goes in v2:
time: 83.5 us; the launch traced here: 83.3 us
  Pallas kernels  82.7 us (99%)
    pallas_call x1, Pallas kernels, local(): pl.pallas_call(kernel, out_shape=shapes, in_specs=[hbm] * 8, out_specs=(v...  81.5 us

profile of v2, /device:TPU:1, one launch (start us, length us, event | category | flops | bytes accessed | tf_op | source)
XLA Modules:
  0.0 83.3 jit_solution(8972544125992571382)
XLA Ops:
  0.6 81.5 %shard_map.127 = (bf16[6,34944]{1,0:T(8,128)(2,1)S(1)}, bf16[6,34944]{1,0:T(8,128)(2,1)S(1)}, f32[91,728]{1,0:T(8,128)S(1)}, f32[9,91]{1,0:T(8,128)S(1)}, f32[1,91]{1,0:T(1,128)S(1)}, /*index=5*/f32[1,91]{1,0:T(1,128)S(1)}) custom-call(bf16[6,34944]{1,0:T(8,128)(2,1)} %bitcast.8, bf16[6,34944]{1,0:T(8,128)(2,1)} %bitcast.9, s32[6,1,48]{2,1,0:T(1,128)} %bitcast.10, ...), custom_call_target="tpu_custom_call" | custom-call | tf_op jit(solution)/shard_map/pallas_call | solution.py:551
  82.2 1.1 %shard_map.128 = (bf16[6,34944]{1,0:T(8,128)(2,1)}, bf16[6,34944]{1,0:T(8,128)(2,1)}, f32[91,728]{1,0:T(8,128)}, f32[9,91]{1,0:T(8,128)}, f32[1,91]{1,0:T(1,128)}, /*index=5*/f32[1,91]{1,0:T(1,128)}) custom-call(bf16[6,34944]{1,0:T(8,128)(2,1)S(1)} %get-tuple-element.18.refs_0_, bf16[6,34944]{1,0:T(8,128)(2,1)S(1)} %get-tuple-element.19.refs_1_, ...), custom_call_target="tpu_custom_call" | custom-call | tf_op jit(solution)/shard_map/pallas_call | solution.py:620
